TPU v7x, 32 devices: a whole 2x2x4 slice. The times are simulated.
32 devices in a mesh: outer: 8 (over z, x), inner: 4 (over y, core).
Axes of the slice: x: 2, y: 2, z: 4, core: 2. Of those that a mesh axis runs over, the one named last changes fastest.
Arguments:
- queries: bfloat16 [1024, 2, 4096], P('outer', None, 'inner'), may hold values from -52 to 52
- keys: bfloat16 [1024, 2, 4096], P('outer', None, 'inner'), may hold values from -6 to 6
- values: bfloat16 [1024, 2, 4096], P('outer', None, 'inner'), may hold values from -6 to 6
Outputs:
- attended: bfloat16 [1024, 2, 4096], P(('outer', 'inner'))
All inputs are finite; a program needn't handle non-finite values.
Results may differ from a plain program's by a relative error of at most 0.004.
Values may be sent and summed in bfloat16 or wider, within the bound.
A program may use at most 128 MiB of HBM per device.

v0:
```python
from functools import partial
import math

import jax
import jax.numpy as jnp
from jax import lax
from jax.experimental import pallas as pl
from jax.experimental.pallas import tpu as pltpu
from jax.sharding import PartitionSpec as P

HEAD_DIM = 128
MESH = pl.DeviceIdType.MESH


def attend_keys(running, key_block, value_block, query_heads, head_count):
    peak_rows, totals, numerator = running
    key_count = key_block.shape[0]
    key_heads = key_block.reshape(key_count, head_count, HEAD_DIM)
    value_heads = value_block.reshape(key_count, head_count, HEAD_DIM)
    scores = jnp.einsum(
        "qhd,khd->qhk", query_heads, key_heads, preferred_element_type=jnp.float32
    ) * (1.0 / math.sqrt(HEAD_DIM))
    new_peaks = jnp.maximum(peak_rows, jnp.max(scores, axis=2))
    shrink = jnp.exp(peak_rows - new_peaks)
    weights = jnp.exp(scores - new_peaks[..., None])
    totals = totals * shrink + jnp.sum(weights, axis=2)
    numerator = numerator * shrink[..., None] + jnp.einsum(
        "qhk,khd->qhd",
        weights.astype(jnp.bfloat16),
        value_heads,
        preferred_element_type=jnp.float32,
    )
    return (new_peaks, totals, numerator)


def attend_piece(running, pieces, query_part, head_count):
    key_rows, value_rows = pieces
    row_count = query_part.shape[0]
    query_heads = query_part.reshape(row_count, head_count, HEAD_DIM)
    block_count = key_rows.shape[0] // row_count
    key_blocks = key_rows.reshape(block_count, row_count, key_rows.shape[1])
    value_blocks = value_rows.reshape(block_count, row_count, value_rows.shape[1])

    def one_block(state, blocks):
        return (attend_keys(state, blocks[0], blocks[1], query_heads, head_count), None)

    running, unused = lax.scan(one_block, running, (key_blocks, value_blocks))
    return running


def start_state(row_count, head_count):
    peak_rows = jnp.full((row_count, head_count), -jnp.inf, jnp.float32)
    totals = jnp.zeros((row_count, head_count), jnp.float32)
    numerator = jnp.zeros((row_count, head_count, HEAD_DIM), jnp.float32)
    return (peak_rows, totals, numerator)


def finish_state(running):
    peak_rows, totals, numerator = running
    averaged = numerator / totals[..., None]
    return averaged.reshape(numerator.shape[0], -1).astype(jnp.bfloat16)


def flatten(array):
    return array.reshape(array.shape[0], array.shape[1] * array.shape[2])


def per_device_split(queries, keys, values):
    tok_rows, networks, local_cols = queries.shape
    full_q, full_k, full_v = (
        lax.all_to_all(array, "inner", split_axis=0, concat_axis=2, tiled=True)
        for array in (queries, keys, values)
    )
    unit_rows = full_q.shape[0]
    full_cols = full_q.shape[2]
    query_part, key_part, value_part = (
        lax.all_to_all(flatten(array), "outer", split_axis=1, concat_axis=0, tiled=True)
        for array in (full_q, full_k, full_v)
    )
    head_count = query_part.shape[1] // HEAD_DIM
    running = attend_piece(
        start_state(query_part.shape[0], head_count),
        (
            lax.all_gather(key_part, "inner", axis=0, tiled=True),
            lax.all_gather(value_part, "inner", axis=0, tiled=True),
        ),
        query_part,
        head_count,
    )
    gathered = lax.all_to_all(
        finish_state(running), "outer", split_axis=0, concat_axis=1, tiled=True
    )
    return gathered.reshape(unit_rows, networks, full_cols)


def attend_block(query, key, value):
    raw = lax.dot_general(
        query, key, (((1,), (1,)), ((), ())), preferred_element_type=jnp.float32
    )
    peak = jnp.max(raw, axis=1, keepdims=True)
    weights = jnp.exp2((raw - peak) * (math.log2(math.e) / math.sqrt(HEAD_DIM)))
    totals = jnp.sum(weights, axis=1, keepdims=True)
    numerator = jnp.dot(
        weights.astype(jnp.bfloat16), value, preferred_element_type=jnp.float32
    )
    return (numerator / totals).astype(jnp.bfloat16)


def exchange_kernel(
    outer, inner, heads,
    q_ref, k_ref, v_ref, out_ref,
    q_raw, k_raw, v_raw, k_buf, v_buf, o_raw,
    q_src, k_src, v_src, src_sem, local_sem, in_send, in_recv, out_send, out_recv,
):
    me_o, me_i = lax.axis_index("outer"), lax.axis_index("inner")
    tokens, networks, local_cols = q_ref.shape
    out_rows = out_ref.shape[0]
    half = outer // 2
    my_half, my_rest = me_o // half, me_o % half
    refs, raws = (k_src, v_src, q_src), (k_raw, v_raw, q_raw)

    def partner(step, sign):
        side = jnp.where(step < half, 1 - my_half, my_half)
        return side * half + (my_rest + sign * step + 2 * outer) % half

    def rows_of(block):
        return pl.ds(pl.multiple_of(block * tokens, tokens), tokens)

    def cols_of(head):
        return pl.ds(pl.multiple_of(head * HEAD_DIM, HEAD_DIM), HEAD_DIM)

    steps = [step for step in range(outer) if step != half]

    def in_copy(head, which, step, sign):
        other = partner(step, sign)
        target = other if sign == 1 else me_o
        source = me_o if sign == 1 else other
        return pltpu.make_async_remote_copy(
            src_ref=refs[which].at[:, :, cols_of(target * heads + head)],
            dst_ref=raws[which].at[head, rows_of(source)],
            send_sem=in_send,
            recv_sem=in_recv.at[head * 3 + which, step],
            device_id=(other, me_i),
            device_id_type=MESH,
        )

    def own_copy(head, which):
        return pltpu.make_async_copy(
            refs[which].at[:, :, cols_of(me_o * heads + head)],
            raws[which].at[head, rows_of(me_o)],
            local_sem.at[head * 3 + which],
        )

    def out_cols(source_o, source_i, head):
        return cols_of(source_i * (local_cols // HEAD_DIM) + source_o * heads + head)

    def out_slice(block, part):
        return pl.ds(block * tokens + part * out_rows, out_rows)

    def out_copy(head, block, part):
        return pltpu.make_async_remote_copy(
            src_ref=o_raw.at[head, out_slice(block, part)],
            dst_ref=out_ref.at[:, :, out_cols(me_o, me_i, head)],
            send_sem=out_send,
            recv_sem=out_recv,
            device_id=(block, part),
            device_id_type=MESH,
        )

    def out_own(head):
        return pltpu.make_async_copy(
            o_raw.at[head, out_slice(me_o, me_i)],
            out_ref.at[:, :, out_cols(me_o, me_i, head)],
            out_recv,
        )

    barrier = pltpu.get_barrier_semaphore()

    sources = [
        pltpu.make_async_copy(ref, kept, src_sem.at[which])
        for which, (ref, kept) in enumerate(zip((k_ref, v_ref, q_ref), refs))
    ]
    for copy in sources:
        copy.start()
    ends = [partner(step, 1) for step in steps]
    for shift in range(inner):
        part = (me_i + shift) % inner
        for other in ends:
            pl.semaphore_signal(barrier, inc=1, device_id=(other, part), device_id_type=MESH)
        if shift:
            pl.semaphore_signal(barrier, inc=1, device_id=(me_o, part), device_id_type=MESH)
    for copy in sources:
        copy.wait()
    pl.semaphore_wait(barrier, outer * inner - 1)

    for head in range(heads):
        for which in range(3):
            for step in steps:
                in_copy(head, which, step, 1).start()
            own_copy(head, which).start()

    both = networks * tokens
    split_row = lax.broadcasted_iota(jnp.int32, (both, both), 0)
    split_col = lax.broadcasted_iota(jnp.int32, (both, both), 1)
    split = (split_col == (split_row % tokens) * networks + split_row // tokens)
    split = split.astype(jnp.float32).astype(jnp.bfloat16)
    join = (split_row == (split_col % tokens) * networks + split_col // tokens)
    join = join.astype(jnp.float32).astype(jnp.bfloat16)

    def separate(raw, head, block):
        mixed = raw[head, rows_of(block)].reshape(both, HEAD_DIM)
        return jnp.dot(split, mixed, preferred_element_type=jnp.float32).astype(jnp.bfloat16)

    def place(head, which, block):
        apart = separate(raws[which], head, block)
        kept = (k_buf, v_buf)[which]
        for network in range(networks):
            kept[network, rows_of(block)] = apart[network * tokens:(network + 1) * tokens]

    def compute(head, block):
        query = separate(q_raw, head, block)
        parts = [
            attend_block(query[n * tokens:(n + 1) * tokens], k_buf[n], v_buf[n])
            for n in range(networks)
        ]
        mixed = jnp.dot(join, jnp.concatenate(parts, axis=0), preferred_element_type=jnp.float32)
        o_raw[head, rows_of(block)] = mixed.astype(jnp.bfloat16).reshape(
            tokens, networks, HEAD_DIM
        )

    for head in range(heads):
        for which in range(3):
            own_copy(head, which).wait()
        for which in range(2):
            place(head, which, me_o)

            def one_place(index, carry):
                step = jnp.where(index < half, index, index + 1)
                in_copy(head, which, step, -1).wait_recv()
                place(head, which, partner(step, -1))
                return carry

            lax.fori_loop(0, outer - 1, one_place, 0)

        compute(head, me_o)
        for shift in range(1, inner):
            out_copy(head, me_o, (me_i + shift) % inner).start()
        out_own(head).start()

        def one_block(index, carry):
            step = jnp.where(index < half, index, index + 1)
            in_copy(head, 2, step, -1).wait_recv()
            block = partner(step, -1)
            compute(head, block)
            for part in range(inner):
                out_copy(head, block, part).start()
            return carry

        lax.fori_loop(0, outer - 1, one_block, 0)

    def wait_bytes(ref, sem):
        pltpu.make_async_copy(ref, ref, sem).wait()

    for head in range(heads):
        for raw in raws:
            wait_bytes(raw.at[head, pl.ds(0, tokens * (outer - 1))], in_send)
        wait_bytes(o_raw.at[head, pl.ds(0, tokens * outer - out_rows)], out_send)
    wait_bytes(out_ref, out_recv)


def per_device(outer, inner, queries, keys, values):
    tokens, networks, local_cols = queries.shape
    heads = local_cols // HEAD_DIM // outer
    seq = tokens * outer
    out_rows = tokens // inner
    raw = pltpu.VMEM((heads, seq, networks, HEAD_DIM), jnp.bfloat16)
    kept = pltpu.VMEM((networks, seq, HEAD_DIM), jnp.bfloat16)
    return pl.pallas_call(
        partial(exchange_kernel, outer, inner, heads),
        out_shape=jax.ShapeDtypeStruct((out_rows, networks, local_cols * inner), jnp.bfloat16),
        in_specs=[pl.BlockSpec(memory_space=pl.ANY)] * 3,
        out_specs=pl.BlockSpec(memory_space=pl.ANY),
        scratch_shapes=[
            raw, raw, raw, kept, kept, raw,
            *[pltpu.VMEM(queries.shape, jnp.bfloat16)] * 3,
            pltpu.SemaphoreType.DMA((3,)),
            pltpu.SemaphoreType.DMA((heads * 3,)),
            pltpu.SemaphoreType.DMA,
            pltpu.SemaphoreType.DMA((heads * 3, outer)),
            pltpu.SemaphoreType.DMA,
            pltpu.SemaphoreType.DMA,
        ],
        compiler_params=pltpu.CompilerParams(collective_id=0, has_side_effects=True, vmem_limit_bytes=54500 * 1024),
    )(queries, keys, values)


def solution(mesh):
    outer, inner = mesh.shape["outer"], mesh.shape["inner"]

    def body(queries, keys, values):
        heads = queries.shape[2] // HEAD_DIM
        if outer % 2 == 0 and heads % outer == 0:
            return per_device(outer, inner, queries, keys, values)
        return per_device_split(queries, keys, values)

    return jax.shard_map(
        body,
        mesh=mesh,
        in_specs=(P("outer", None, "inner"),) * 3,
        out_specs=P(("outer", "inner"), None, None),
        check_vma=False,
    )
```

profile of v0, /device:TPU:25, one launch (start us, length us, event | category | flops | bytes accessed | tf_op | source)
XLA Modules:
  0.0 55.3 jit_solution(8641165062664368430)
XLA Ops:
  0.0 54.5 %shard_map.37 = bf16[32,2,4096]{2,1,0:T(2,128)(2,1)S(1)} custom-call(bf16[128,2,1024]{2,1,0:T(2,128)(2,1)} %q_ref.1, bf16[128,2,1024]{2,1,0:T(2,128)(2,1)} %k_ref.1, bf16[128,2,1024]{2,1,0:T(2,128)(2,1)} %v_ref.1), custom_call_target="tpu_custom_call" | custom-call | tf_op jit(solution)/shard_map/pallas_call | solution.py:278
  54.5 0.8 %copy.5 = bf16[32,2,4096]{2,1,0:T(2,128)(2,1)} copy(bf16[32,2,4096]{2,1,0:T(2,128)(2,1)S(1)} %shard_map.37) | data formatting | bytes 1048576
where the time goes:
time: 55.5 us; the launch traced here: 55.3 us
  Pallas kernels  54.5 us (98%)
  local copies, waits for them, and re-layouts  0.8 us (1%)
    pallas_call x1, Pallas kernels, per_device(): pl.pallas_call(partial(exchange_kernel, outer, inner, heads), out_shape=j...  54.5 us

commit v1 on v0

--- a/solution.py
+++ b/solution.py
@@ -106,22 +106,47 @@
     return (numerator / totals).astype(jnp.bfloat16)
 
 
+COLUMNS = 2
+
+
 def exchange_kernel(
     outer, inner, heads,
     q_ref, k_ref, v_ref, out_ref,
     q_raw, k_raw, v_raw, k_buf, v_buf, o_raw,
-    q_src, k_src, v_src, src_sem, local_sem, in_send, in_recv, out_send, out_recv,
+    q_src, k_src, v_src, src_sem, local_sem, in_send, in_recv, out_send, out_recv, ready,
 ):
     me_o, me_i = lax.axis_index("outer"), lax.axis_index("inner")
     tokens, networks, local_cols = q_ref.shape
     out_rows = out_ref.shape[0]
-    half = outer // 2
-    my_half, my_rest = me_o // half, me_o % half
+    rows, half = outer // COLUMNS, outer // COLUMNS // 2
+    row, col = me_o // COLUMNS, me_o % COLUMNS
+    near_side = half * COLUMNS - 1
     refs, raws = (k_src, v_src, q_src), (k_raw, v_raw, q_raw)
 
-    def partner(step, sign):
-        side = jnp.where(step < half, 1 - my_half, my_half)
-        return side * half + (my_rest + sign * step + 2 * outer) % half
+    def peer(slot, row, col, where):
+        side = row // half
+        turn = slot + 1
+        same = side * half + (row + turn // COLUMNS) % half
+        away = (slot - near_side) // COLUMNS
+        other = where(side == 0, half + away, half - 1 - away)
+        is_near = slot < near_side
+        shift = where(is_near, turn, slot - near_side)
+        return where(is_near, same, other), (col + shift) % COLUMNS
+
+    def pick(test, yes, no):
+        return yes if test else no
+
+    def distances(slot):
+        found = set()
+        for r in range(rows):
+            for c in range(COLUMNS):
+                pr, pc = peer(slot, r, c, pick)
+                found.add(abs(pr - r) + abs(pc - c))
+        return sorted(found)
+
+    def traced_peer(slot):
+        pr, pc = peer(slot, row, col, jnp.where)
+        return pr * COLUMNS + pc, jnp.abs(pr - row) + jnp.abs(pc - col)
 
     def rows_of(block):
         return pl.ds(pl.multiple_of(block * tokens, tokens), tokens)
@@ -129,20 +154,21 @@
     def cols_of(head):
         return pl.ds(pl.multiple_of(head * HEAD_DIM, HEAD_DIM), HEAD_DIM)
 
-    steps = [step for step in range(outer) if step != half]
-
-    def in_copy(head, which, step, sign):
-        other = partner(step, sign)
-        target = other if sign == 1 else me_o
-        source = me_o if sign == 1 else other
+    def in_copy(head, which, target, source, other):
         return pltpu.make_async_remote_copy(
             src_ref=refs[which].at[:, :, cols_of(target * heads + head)],
             dst_ref=raws[which].at[head, rows_of(source)],
             send_sem=in_send,
-            recv_sem=in_recv.at[head * 3 + which, step],
+            recv_sem=in_recv.at[head * 3 + which, source],
             device_id=(other, me_i),
             device_id_type=MESH,
         )
+
+    def send_in(head, which, other):
+        in_copy(head, which, other, me_o, other).start()
+
+    def wait_in(head, which, source):
+        in_copy(head, which, me_o, source, source).wait_recv()
 
     def own_copy(head, which):
         return pltpu.make_async_copy(
@@ -174,30 +200,68 @@
             out_recv,
         )
 
+    def tell(sem, device):
+        pl.semaphore_signal(sem, inc=1, device_id=device, device_id_type=MESH)
+
+    beside = [
+        (row > 0, me_o - COLUMNS),
+        (row < rows - 1, me_o + COLUMNS),
+        (col > 0, me_o - 1),
+        (col < COLUMNS - 1, me_o + 1),
+    ]
+    beside_count = sum(jnp.where(exists, 1, 0) for exists, other in beside)
+
+    def tell_beside(sem):
+        for exists, other in beside:
+            @pl.when(exists)
+            def _():
+                tell(sem, (other, me_i))
+
+    def meet(round_at):
+        tell_beside(ready.at[round_at])
+        pl.semaphore_wait(ready.at[round_at], beside_count)
+
     barrier = pltpu.get_barrier_semaphore()
-
+    tell_beside(barrier)
+    for shift in range(1, inner):
+        tell(barrier, (me_o, (me_i + shift) % inner))
     sources = [
         pltpu.make_async_copy(ref, kept, src_sem.at[which])
         for which, (ref, kept) in enumerate(zip((k_ref, v_ref, q_ref), refs))
     ]
     for copy in sources:
         copy.start()
-    ends = [partner(step, 1) for step in steps]
-    for shift in range(inner):
-        part = (me_i + shift) % inner
-        for other in ends:
-            pl.semaphore_signal(barrier, inc=1, device_id=(other, part), device_id_type=MESH)
-        if shift:
-            pl.semaphore_signal(barrier, inc=1, device_id=(me_o, part), device_id_type=MESH)
-    for copy in sources:
+    for copy in sources[:2]:
         copy.wait()
-    pl.semaphore_wait(barrier, outer * inner - 1)
-
+    pl.semaphore_wait(barrier, beside_count + inner - 1)
+
+    slots = [*range(near_side, outer - 1), *range(near_side)]
+    furthest = rows + COLUMNS - 2
+    for reach in range(1, furthest + 1):
+        if reach > 1:
+            meet(reach - 2)
+        for slot in slots:
+            lengths = distances(slot)
+            if reach not in lengths:
+                continue
+            other, length = traced_peer(slot)
+
+            def send_pair():
+                for which in range(2):
+                    send_in(0, which, other)
+
+            if len(lengths) == 1:
+                send_pair()
+            else:
+                pl.when(length == reach)(send_pair)
+    sources[2].wait()
     for head in range(heads):
         for which in range(3):
-            for step in steps:
-                in_copy(head, which, step, 1).start()
+            if head or which == 2:
+                for slot in range(outer - 1):
+                    send_in(head, which, traced_peer(slot)[0])
             own_copy(head, which).start()
+    meet(furthest - 1)
 
     both = networks * tokens
     split_row = lax.broadcasted_iota(jnp.int32, (both, both), 0)
@@ -234,23 +298,23 @@
         for which in range(2):
             place(head, which, me_o)
 
-            def one_place(index, carry):
-                step = jnp.where(index < half, index, index + 1)
-                in_copy(head, which, step, -1).wait_recv()
-                place(head, which, partner(step, -1))
-                return carry
-
-            lax.fori_loop(0, outer - 1, one_place, 0)
+        def one_place(slot, carry):
+            block = traced_peer(slot)[0]
+            for which in range(2):
+                wait_in(head, which, block)
+                place(head, which, block)
+            return carry
+
+        lax.fori_loop(0, outer - 1, one_place, 0)
 
         compute(head, me_o)
         for shift in range(1, inner):
             out_copy(head, me_o, (me_i + shift) % inner).start()
         out_own(head).start()
 
-        def one_block(index, carry):
-            step = jnp.where(index < half, index, index + 1)
-            in_copy(head, 2, step, -1).wait_recv()
-            block = partner(step, -1)
+        def one_block(slot, carry):
+            block = traced_peer(slot)[0]
+            wait_in(head, 2, block)
             compute(head, block)
             for part in range(inner):
                 out_copy(head, block, part).start()
@@ -289,6 +353,7 @@
             pltpu.SemaphoreType.DMA((heads * 3, outer)),
             pltpu.SemaphoreType.DMA,
             pltpu.SemaphoreType.DMA,
+            pltpu.SemaphoreType.REGULAR((outer // COLUMNS + COLUMNS - 2,)),
         ],
         compiler_params=pltpu.CompilerParams(collective_id=0, has_side_effects=True, vmem_limit_bytes=54500 * 1024),
     )(queries, keys, values)
@@ -299,7 +364,7 @@
 
     def body(queries, keys, values):
         heads = queries.shape[2] // HEAD_DIM
-        if outer % 2 == 0 and heads % outer == 0:
+        if outer % (2 * COLUMNS) == 0 and heads % outer == 0:
             return per_device(outer, inner, queries, keys, values)
         return per_device_split(queries, keys, values)
 

time: 55.5 us -> 54 us (0.973)
  the two profiles are of different devices: /device:TPU:25 before, /device:TPU:0 now
where the time goes in v1:
time: 54 us; the launch traced here: 53.8 us
  Pallas kernels  53 us (98%)
  local copies, waits for them, and re-layouts  0.8 us (1%)
    pallas_call x1, Pallas kernels, per_device(): pl.pallas_call(partial(exchange_kernel, outer, inner, heads), out_shape=j...  53 us

profile of v1, /device:TPU:0, one launch (start us, length us, event | category | flops | bytes accessed | tf_op | source)
XLA Modules:
  0.0 53.8 jit_solution(2100877821771404017)
XLA Ops:
  0.0 53.0 %shard_map.37 = bf16[32,2,4096]{2,1,0:T(2,128)(2,1)S(1)} custom-call(bf16[128,2,1024]{2,1,0:T(2,128)(2,1)} %q_ref.1, bf16[128,2,1024]{2,1,0:T(2,128)(2,1)} %k_ref.1, bf16[128,2,1024]{2,1,0:T(2,128)(2,1)} %v_ref.1), custom_call_target="tpu_custom_call" | custom-call | tf_op jit(solution)/shard_map/pallas_call | solution.py:342
  53.0 0.8 %copy.5 = bf16[32,2,4096]{2,1,0:T(2,128)(2,1)} copy(bf16[32,2,4096]{2,1,0:T(2,128)(2,1)S(1)} %shard_map.37) | data formatting | bytes 1048576

commit v2 on v1

--- a/solution.py
+++ b/solution.py
@@ -136,9 +136,9 @@
     def pick(test, yes, no):
         return yes if test else no
 
-    def distances(slot):
+    def distances(slot, chosen_rows):
         found = set()
-        for r in range(rows):
+        for r in chosen_rows:
             for c in range(COLUMNS):
                 pr, pc = peer(slot, r, c, pick)
                 found.add(abs(pr - r) + abs(pc - c))
@@ -231,36 +231,53 @@
     ]
     for copy in sources:
         copy.start()
-    for copy in sources[:2]:
+    for copy in sources:
         copy.wait()
     pl.semaphore_wait(barrier, beside_count + inner - 1)
 
-    slots = [*range(near_side, outer - 1), *range(near_side)]
+    near_slots, away_slots = range(near_side), range(near_side, outer - 1)
+    central = jnp.abs(2 * row - (rows - 1)) == 1
+    central_rows = (half - 1, half)
+    outward_rows = [r for r in range(rows) if r not in central_rows]
     furthest = rows + COLUMNS - 2
+
+    def send_at(reach, slots, sent, chosen_rows, chosen=None):
+        for slot in slots:
+            lengths = distances(slot, chosen_rows)
+            if reach not in lengths:
+                continue
+            other, length = traced_peer(slot)
+            test = chosen
+            if len(lengths) > 1:
+                near_enough = length == reach
+                test = near_enough if test is None else jnp.logical_and(test, near_enough)
+
+            def send():
+                for which in sent:
+                    send_in(0, which, other)
+
+            if test is None:
+                send()
+            else:
+                pl.when(test)(send)
+
+    def send_queries(head):
+        for slot in away_slots:
+            send_in(head, 2, traced_peer(slot)[0])
+
+    outward = jnp.logical_not(central)
     for reach in range(1, furthest + 1):
         if reach > 1:
             meet(reach - 2)
-        for slot in slots:
-            lengths = distances(slot)
-            if reach not in lengths:
-                continue
-            other, length = traced_peer(slot)
-
-            def send_pair():
-                for which in range(2):
-                    send_in(0, which, other)
-
-            if len(lengths) == 1:
-                send_pair()
-            else:
-                pl.when(length == reach)(send_pair)
-    sources[2].wait()
+        send_at(reach, away_slots, (0, 1), central_rows, central)
+        send_at(reach, near_slots, (0, 1, 2), range(rows))
+        send_at(reach, away_slots, (0, 1), outward_rows, outward)
+    pl.when(outward)(partial(send_queries, 0))
     for head in range(heads):
         for which in range(3):
-            if head or which == 2:
-                for slot in range(outer - 1):
-                    send_in(head, which, traced_peer(slot)[0])
             own_copy(head, which).start()
+            for slot in range(outer - 1) if head else ():
+                send_in(head, which, traced_peer(slot)[0])
     meet(furthest - 1)
 
     both = networks * tokens
@@ -306,13 +323,16 @@
             return carry
 
         lax.fori_loop(0, outer - 1, one_place, 0)
+        if head == 0:
+            pl.when(central)(partial(send_queries, 0))
 
         compute(head, me_o)
         for shift in range(1, inner):
             out_copy(head, me_o, (me_i + shift) % inner).start()
         out_own(head).start()
 
-        def one_block(slot, carry):
+        def one_block(index, carry):
+            slot = jnp.where(index < near_side, index, outer - 2 + near_side - index)
             block = traced_peer(slot)[0]
             wait_in(head, 2, block)
             compute(head, block)

time: 54 us -> 51.3 us (0.950)
  Pallas kernels: 53 us -> 50.3 us
    pallas_call x1, Pallas kernels: 53 us -> 50.3 us  [per_device(): pl.pallas_call(partial(exchange_kernel, outer, inner, heads), out_shape=j...]
where the time goes in v2:
time: 51.3 us; the launch traced here: 51.1 us
  Pallas kernels  50.3 us (98%)
  local copies, waits for them, and re-layouts  0.8 us (2%)
    pallas_call x1, Pallas kernels, per_device(): pl.pallas_call(partial(exchange_kernel, outer, inner, heads), out_shape=j...  50.3 us

profile of v2, /device:TPU:0, one launch (start us, length us, event | category | flops | bytes accessed | tf_op | source)
XLA Modules:
  0.0 51.1 jit_solution(15336281050999769557)
XLA Ops:
  0.0 50.3 %shard_map.37 = bf16[32,2,4096]{2,1,0:T(2,128)(2,1)S(1)} custom-call(bf16[128,2,1024]{2,1,0:T(2,128)(2,1)} %q_ref.1, bf16[128,2,1024]{2,1,0:T(2,128)(2,1)} %k_ref.1, bf16[128,2,1024]{2,1,0:T(2,128)(2,1)} %v_ref.1), custom_call_target="tpu_custom_call" | custom-call | tf_op jit(solution)/shard_map/pallas_call | solution.py:362
  50.3 0.8 %copy.5 = bf16[32,2,4096]{2,1,0:T(2,128)(2,1)} copy(bf16[32,2,4096]{2,1,0:T(2,128)(2,1)S(1)} %shard_map.37) | data formatting | bytes 1048576

commit v3 on v2

--- a/solution.py
+++ b/solution.py
@@ -113,7 +113,7 @@
     outer, inner, heads,
     q_ref, k_ref, v_ref, out_ref,
     q_raw, k_raw, v_raw, k_buf, v_buf, o_raw,
-    q_src, k_src, v_src, src_sem, local_sem, in_send, in_recv, out_send, out_recv, ready,
+    q_src, k_src, v_src, src_sem, local_sem, in_send, in_recv, out_send, out_recv, answer, ready,
 ):
     me_o, me_i = lax.axis_index("outer"), lax.axis_index("inner")
     tokens, networks, local_cols = q_ref.shape
@@ -121,6 +121,7 @@
     rows, half = outer // COLUMNS, outer // COLUMNS // 2
     row, col = me_o // COLUMNS, me_o % COLUMNS
     near_side = half * COLUMNS - 1
+    furthest = rows + COLUMNS - 2
     refs, raws = (k_src, v_src, q_src), (k_raw, v_raw, q_raw)
 
     def peer(slot, row, col, where):
@@ -218,28 +219,45 @@
                 tell(sem, (other, me_i))
 
     def meet(round_at):
-        tell_beside(ready.at[round_at])
         pl.semaphore_wait(ready.at[round_at], beside_count)
-
-    barrier = pltpu.get_barrier_semaphore()
-    tell_beside(barrier)
-    for shift in range(1, inner):
-        tell(barrier, (me_o, (me_i + shift) % inner))
+        if round_at < furthest - 1:
+            tell_beside(ready.at[round_at + 1])
+
     sources = [
         pltpu.make_async_copy(ref, kept, src_sem.at[which])
         for which, (ref, kept) in enumerate(zip((k_ref, v_ref, q_ref), refs))
     ]
+    barrier = pltpu.get_barrier_semaphore()
+    facing = row + 1 == half
+    greeted = [(row < rows - 1, (me_o + COLUMNS, me_i)), (col < COLUMNS - 1, (me_o + 1, me_i))]
+    answered = [
+        (jnp.logical_and(row > 0, row != half), (me_o - COLUMNS, me_i)),
+        (col > 0, (me_o - 1, me_i)),
+    ]
+    for part in range(inner):
+        greeted.append((part > me_i, (me_o, part)))
+        answered.append((part < me_i, (me_o, part)))
+    greeted.append((row == half, (me_o - COLUMNS, me_i)))
+
+    def tell_those(sem, those):
+        for exists, device in those:
+            pl.when(exists)(partial(tell, sem, device))
+
+    def count(*tests):
+        return sum(jnp.where(test, 1, 0) for test in tests)
+
+    def wait_for(sem, amount):
+        pl.when(amount > 0)(lambda: pl.semaphore_wait(sem, amount))
+
+    tell_those(barrier, greeted)
     for copy in sources:
         copy.start()
-    for copy in sources:
-        copy.wait()
-    pl.semaphore_wait(barrier, beside_count + inner - 1)
-
+    wait_for(barrier, count(row > 0, col > 0, facing) + me_i)
+    tell_those(answer, answered)
     near_slots, away_slots = range(near_side), range(near_side, outer - 1)
     central = jnp.abs(2 * row - (rows - 1)) == 1
     central_rows = (half - 1, half)
     outward_rows = [r for r in range(rows) if r not in central_rows]
-    furthest = rows + COLUMNS - 2
 
     def send_at(reach, slots, sent, chosen_rows, chosen=None):
         for slot in slots:
@@ -261,18 +279,27 @@
             else:
                 pl.when(test)(send)
 
-    def send_queries(head):
-        for slot in away_slots:
+    def send_queries(head, slots):
+        for slot in slots:
             send_in(head, 2, traced_peer(slot)[0])
 
     outward = jnp.logical_not(central)
+    facing_slot = (near_side,)
+    away_slots_left = range(near_side + 1, outer - 1)
+    for which in range(2):
+        sources[which].wait()
+        send_at(1, facing_slot, (which,), central_rows, central)
+    sources[2].wait()
+    above = jnp.logical_and(row < rows - 1, jnp.logical_not(facing))
+    wait_for(answer, count(above, col < COLUMNS - 1) + inner - 1 - me_i)
+    tell_beside(ready.at[0])
     for reach in range(1, furthest + 1):
         if reach > 1:
             meet(reach - 2)
-        send_at(reach, away_slots, (0, 1), central_rows, central)
+        send_at(reach, away_slots_left, (0, 1), central_rows, central)
         send_at(reach, near_slots, (0, 1, 2), range(rows))
         send_at(reach, away_slots, (0, 1), outward_rows, outward)
-    pl.when(outward)(partial(send_queries, 0))
+    pl.when(outward)(partial(send_queries, 0, away_slots))
     for head in range(heads):
         for which in range(3):
             own_copy(head, which).start()
@@ -324,7 +351,7 @@
 
         lax.fori_loop(0, outer - 1, one_place, 0)
         if head == 0:
-            pl.when(central)(partial(send_queries, 0))
+            pl.when(central)(partial(send_queries, 0, away_slots))
 
         compute(head, me_o)
         for shift in range(1, inner):
@@ -373,6 +400,7 @@
             pltpu.SemaphoreType.DMA((heads * 3, outer)),
             pltpu.SemaphoreType.DMA,
             pltpu.SemaphoreType.DMA,
+            pltpu.SemaphoreType.REGULAR,
             pltpu.SemaphoreType.REGULAR((outer // COLUMNS + COLUMNS - 2,)),
         ],
         compiler_params=pltpu.CompilerParams(collective_id=0, has_side_effects=True, vmem_limit_bytes=54500 * 1024),

time: 51.3 us -> 50.7 us (0.988)
  Pallas kernels: 50.3 us -> 49.4 us
    pallas_call x1, Pallas kernels: 50.3 us -> 49.4 us  [per_device(): pl.pallas_call(partial(exchange_kernel, outer, inner, heads), out_shape=j...]
where the time goes in v3:
time: 50.7 us; the launch traced here: 50.2 us
  Pallas kernels  49.4 us (97%)
  local copies, waits for them, and re-layouts  0.8 us (2%)
    pallas_call x1, Pallas kernels, per_device(): pl.pallas_call(partial(exchange_kernel, outer, inner, heads), out_shape=j...  49.4 us

profile of v3, /device:TPU:0, one launch (start us, length us, event | category | flops | bytes accessed | tf_op | source)
XLA Modules:
  0.0 50.2 jit_solution(13388287582266301479)
XLA Ops:
  0.0 49.4 %shard_map.37 = bf16[32,2,4096]{2,1,0:T(2,128)(2,1)S(1)} custom-call(bf16[128,2,1024]{2,1,0:T(2,128)(2,1)} %q_ref.1, bf16[128,2,1024]{2,1,0:T(2,128)(2,1)} %k_ref.1, bf16[128,2,1024]{2,1,0:T(2,128)(2,1)} %v_ref.1), custom_call_target="tpu_custom_call" | custom-call | tf_op jit(solution)/shard_map/pallas_call | solution.py:389
  49.4 0.8 %copy.5 = bf16[32,2,4096]{2,1,0:T(2,128)(2,1)} copy(bf16[32,2,4096]{2,1,0:T(2,128)(2,1)S(1)} %shard_map.37) | data formatting | bytes 1048576

commit v4 on v3

--- a/solution.py
+++ b/solution.py
@@ -254,41 +254,38 @@
         copy.start()
     wait_for(barrier, count(row > 0, col > 0, facing) + me_i)
     tell_those(answer, answered)
-    near_slots, away_slots = range(near_side), range(near_side, outer - 1)
+    away_slots = range(near_side, outer - 1)
+    beside_slots = range(COLUMNS - 1)
+    straight_slots = range(COLUMNS - 1, near_side, COLUMNS)
+    turning_slots = [slot for slot in range(near_side) if slot not in straight_slots]
+    corner_slots = turning_slots[COLUMNS - 1:]
     central = jnp.abs(2 * row - (rows - 1)) == 1
     central_rows = (half - 1, half)
     outward_rows = [r for r in range(rows) if r not in central_rows]
 
-    def send_at(reach, slots, sent, chosen_rows, chosen=None):
+    def send_at(reach, slots, sent, chosen_rows, chosen, earliest=1):
         for slot in slots:
             lengths = distances(slot, chosen_rows)
-            if reach not in lengths:
-                continue
             other, length = traced_peer(slot)
-            test = chosen
-            if len(lengths) > 1:
-                near_enough = length == reach
-                test = near_enough if test is None else jnp.logical_and(test, near_enough)
 
             def send():
                 for which in sent:
                     send_in(0, which, other)
 
-            if test is None:
-                send()
-            else:
-                pl.when(test)(send)
+            for far in lengths:
+                if max(far, min(earliest, furthest)) == reach:
+                    whole = len(lengths) == 1
+                    pl.when(chosen if whole else jnp.logical_and(chosen, length == far))(send)
 
     def send_queries(head, slots):
         for slot in slots:
             send_in(head, 2, traced_peer(slot)[0])
 
     outward = jnp.logical_not(central)
-    facing_slot = (near_side,)
     away_slots_left = range(near_side + 1, outer - 1)
     for which in range(2):
         sources[which].wait()
-        send_at(1, facing_slot, (which,), central_rows, central)
+        pl.when(central)(partial(send_in, 0, which, traced_peer(near_side)[0]))
     sources[2].wait()
     above = jnp.logical_and(row < rows - 1, jnp.logical_not(facing))
     wait_for(answer, count(above, col < COLUMNS - 1) + inner - 1 - me_i)
@@ -297,8 +294,11 @@
         if reach > 1:
             meet(reach - 2)
         send_at(reach, away_slots_left, (0, 1), central_rows, central)
-        send_at(reach, near_slots, (0, 1, 2), range(rows))
+        send_at(reach, straight_slots, (0, 1, 2), central_rows, central)
+        send_at(reach, turning_slots, (0, 1, 2), central_rows, central, 3)
+        send_at(reach, (*beside_slots, *straight_slots), (0, 1, 2), outward_rows, outward)
         send_at(reach, away_slots, (0, 1), outward_rows, outward)
+        send_at(reach, corner_slots, (0, 1, 2), outward_rows, outward, 3)
     pl.when(outward)(partial(send_queries, 0, away_slots))
     for head in range(heads):
         for which in range(3):

time: 50.7 us -> 50.3 us (level)
  no operation moved by 1% of the time
where the time goes in v4:
time: 50.3 us; the launch traced here: 50 us
  Pallas kernels  49.2 us (98%)
  local copies, waits for them, and re-layouts  0.8 us (2%)
    pallas_call x1, Pallas kernels, per_device(): pl.pallas_call(partial(exchange_kernel, outer, inner, heads), out_shape=j...  49.2 us

profile of v4, /device:TPU:0, one launch (start us, length us, event | category | flops | bytes accessed | tf_op | source)
XLA Modules:
  0.0 50.0 jit_solution(6586106348386807164)
XLA Ops:
  0.0 49.2 %shard_map.37 = bf16[32,2,4096]{2,1,0:T(2,128)(2,1)S(1)} custom-call(bf16[128,2,1024]{2,1,0:T(2,128)(2,1)} %q_ref.1, bf16[128,2,1024]{2,1,0:T(2,128)(2,1)} %k_ref.1, bf16[128,2,1024]{2,1,0:T(2,128)(2,1)} %v_ref.1), custom_call_target="tpu_custom_call" | custom-call | tf_op jit(solution)/shard_map/pallas_call | solution.py:389
  49.2 0.8 %copy.5 = bf16[32,2,4096]{2,1,0:T(2,128)(2,1)} copy(bf16[32,2,4096]{2,1,0:T(2,128)(2,1)S(1)} %shard_map.37) | data formatting | bytes 1048576

commit v5 on v4

--- a/solution.py
+++ b/solution.py
@@ -107,13 +107,14 @@
 
 
 COLUMNS = 2
+CORES = 2
 
 
 def exchange_kernel(
     outer, inner, heads,
     q_ref, k_ref, v_ref, out_ref,
     q_raw, k_raw, v_raw, k_buf, v_buf, o_raw,
-    q_src, k_src, v_src, src_sem, local_sem, in_send, in_recv, out_send, out_recv, answer, ready,
+    q_src, k_src, v_src, src_sem, local_sem, in_send, in_recv, out_send, out_recv, answer, ready, first_src, first_sem,
 ):
     me_o, me_i = lax.axis_index("outer"), lax.axis_index("inner")
     tokens, networks, local_cols = q_ref.shape
@@ -237,7 +238,7 @@
     for part in range(inner):
         greeted.append((part > me_i, (me_o, part)))
         answered.append((part < me_i, (me_o, part)))
-    greeted.append((row == half, (me_o - COLUMNS, me_i)))
+    greeted.insert(0, (row == half, (me_o - COLUMNS, me_i)))
 
     def tell_those(sem, those):
         for exists, device in those:
@@ -249,9 +250,24 @@
     def wait_for(sem, amount):
         pl.when(amount > 0)(lambda: pl.semaphore_wait(sem, amount))
 
-    tell_those(barrier, greeted)
+    central = jnp.abs(2 * row - (rows - 1)) == 1
+    facing_to = traced_peer(near_side)[0]
+    firsts = [
+        pltpu.make_async_copy(
+            ref.at[:, :, cols_of(facing_to * heads)], first_src.at[which], first_sem.at[which]
+        )
+        for which, ref in enumerate((k_ref, v_ref))
+    ]
+
+    def each_first(act):
+        for first in firsts:
+            act(first)
+
+    tell_those(barrier, greeted[:2])
+    pl.when(central)(lambda: each_first(lambda first: first.start()))
     for copy in sources:
         copy.start()
+    tell_those(barrier, greeted[2:])
     wait_for(barrier, count(row > 0, col > 0, facing) + me_i)
     tell_those(answer, answered)
     away_slots = range(near_side, outer - 1)
@@ -259,7 +275,6 @@
     straight_slots = range(COLUMNS - 1, near_side, COLUMNS)
     turning_slots = [slot for slot in range(near_side) if slot not in straight_slots]
     corner_slots = turning_slots[COLUMNS - 1:]
-    central = jnp.abs(2 * row - (rows - 1)) == 1
     central_rows = (half - 1, half)
     outward_rows = [r for r in range(rows) if r not in central_rows]
 
@@ -283,10 +298,21 @@
 
     outward = jnp.logical_not(central)
     away_slots_left = range(near_side + 1, outer - 1)
-    for which in range(2):
-        sources[which].wait()
-        pl.when(central)(partial(send_in, 0, which, traced_peer(near_side)[0]))
-    sources[2].wait()
+    def send_first():
+        for which in range(2):
+            firsts[which].wait()
+            pltpu.make_async_remote_copy(
+                src_ref=first_src.at[which],
+                dst_ref=raws[which].at[0, rows_of(me_o)],
+                send_sem=in_send,
+                recv_sem=in_recv.at[which, me_o],
+                device_id=(facing_to, me_i),
+                device_id_type=MESH,
+            ).start()
+
+    pl.when(central)(send_first)
+    for copy in sources:
+        copy.wait()
     above = jnp.logical_and(row < rows - 1, jnp.logical_not(facing))
     wait_for(answer, count(above, col < COLUMNS - 1) + inner - 1 - me_i)
     tell_beside(ready.at[0])
@@ -363,8 +389,10 @@
             block = traced_peer(slot)[0]
             wait_in(head, 2, block)
             compute(head, block)
-            for part in range(inner):
-                out_copy(head, block, part).start()
+            for turn in range(inner):
+                chip = (me_i // CORES + 1 + turn // CORES) % (inner // CORES)
+                core = (me_i + 1 + turn) % CORES
+                out_copy(head, block, chip * CORES + core).start()
             return carry
 
         lax.fori_loop(0, outer - 1, one_block, 0)
@@ -402,6 +430,8 @@
             pltpu.SemaphoreType.DMA,
             pltpu.SemaphoreType.REGULAR,
             pltpu.SemaphoreType.REGULAR((outer // COLUMNS + COLUMNS - 2,)),
+            pltpu.VMEM((2, tokens, networks, HEAD_DIM), jnp.bfloat16),
+            pltpu.SemaphoreType.DMA((2,)),
         ],
         compiler_params=pltpu.CompilerParams(collective_id=0, has_side_effects=True, vmem_limit_bytes=54500 * 1024),
     )(queries, keys, values)
@@ -412,7 +442,7 @@
 
     def body(queries, keys, values):
         heads = queries.shape[2] // HEAD_DIM
-        if outer % (2 * COLUMNS) == 0 and heads % outer == 0:
+        if outer % (2 * COLUMNS) == 0 and inner % CORES == 0 and heads % outer == 0:
             return per_device(outer, inner, queries, keys, values)
         return per_device_split(queries, keys, values)
 

time: 50.3 us -> 50.5 us (level)
  no operation moved by 1% of the time
where the time goes in v5:
time: 50.5 us; the launch traced here: 50.3 us
  Pallas kernels  49.5 us (98%)
  local copies, waits for them, and re-layouts  0.8 us (2%)
    pallas_call x1, Pallas kernels, per_device(): pl.pallas_call(partial(exchange_kernel, outer, inner, heads), out_shape=j...  49.5 us

profile of v5, /device:TPU:0, one launch (start us, length us, event | category | flops | bytes accessed | tf_op | source)
XLA Modules:
  0.0 50.3 jit_solution(9538919211527871595)
XLA Ops:
  0.0 49.5 %shard_map.37 = bf16[32,2,4096]{2,1,0:T(2,128)(2,1)S(1)} custom-call(bf16[128,2,1024]{2,1,0:T(2,128)(2,1)} %q_ref.1, bf16[128,2,1024]{2,1,0:T(2,128)(2,1)} %k_ref.1, bf16[128,2,1024]{2,1,0:T(2,128)(2,1)} %v_ref.1), custom_call_target="tpu_custom_call" | custom-call | tf_op jit(solution)/shard_map/pallas_call | solution.py:417
  49.5 0.8 %copy.5 = bf16[32,2,4096]{2,1,0:T(2,128)(2,1)} copy(bf16[32,2,4096]{2,1,0:T(2,128)(2,1)S(1)} %shard_map.37) | data formatting | bytes 1048576

commit v6 on v4

--- a/solution.py
+++ b/solution.py
@@ -278,8 +278,9 @@
                     pl.when(chosen if whole else jnp.logical_and(chosen, length == far))(send)
 
     def send_queries(head, slots):
-        for slot in slots:
-            send_in(head, 2, traced_peer(slot)[0])
+        for first in slots[::COLUMNS]:
+            for turned in reversed(range(COLUMNS)):
+                send_in(head, 2, traced_peer(first + turned)[0])
 
     outward = jnp.logical_not(central)
     away_slots_left = range(near_side + 1, outer - 1)

time: 50.3 us -> 50.3 us (level)
  no operation moved by 1% of the time
where the time goes in v6:
time: 50.3 us; the launch traced here: 50 us
  Pallas kernels  49.2 us (98%)
  local copies, waits for them, and re-layouts  0.8 us (2%)
    pallas_call x1, Pallas kernels, per_device(): pl.pallas_call(partial(exchange_kernel, outer, inner, heads), out_shape=j...  49.2 us

profile of v6, /device:TPU:0, one launch (start us, length us, event | category | flops | bytes accessed | tf_op | source)
XLA Modules:
  0.0 50.0 jit_solution(8852899404352076998)
XLA Ops:
  0.0 49.2 %shard_map.37 = bf16[32,2,4096]{2,1,0:T(2,128)(2,1)S(1)} custom-call(bf16[128,2,1024]{2,1,0:T(2,128)(2,1)} %q_ref.1, bf16[128,2,1024]{2,1,0:T(2,128)(2,1)} %k_ref.1, bf16[128,2,1024]{2,1,0:T(2,128)(2,1)} %v_ref.1), custom_call_target="tpu_custom_call" | custom-call | tf_op jit(solution)/shard_map/pallas_call | solution.py:390
  49.2 0.8 %copy.5 = bf16[32,2,4096]{2,1,0:T(2,128)(2,1)} copy(bf16[32,2,4096]{2,1,0:T(2,128)(2,1)S(1)} %shard_map.37) | data formatting | bytes 1048576

commit v7 on v4

--- a/solution.py
+++ b/solution.py
@@ -237,7 +237,7 @@
     for part in range(inner):
         greeted.append((part > me_i, (me_o, part)))
         answered.append((part < me_i, (me_o, part)))
-    greeted.append((row == half, (me_o - COLUMNS, me_i)))
+    greeted.insert(0, (row == half, (me_o - COLUMNS, me_i)))
 
     def tell_those(sem, those):
         for exists, device in those:
@@ -249,9 +249,10 @@
     def wait_for(sem, amount):
         pl.when(amount > 0)(lambda: pl.semaphore_wait(sem, amount))
 
-    tell_those(barrier, greeted)
+    tell_those(barrier, greeted[:2])
     for copy in sources:
         copy.start()
+    tell_those(barrier, greeted[2:])
     wait_for(barrier, count(row > 0, col > 0, facing) + me_i)
     tell_those(answer, answered)
     away_slots = range(near_side, outer - 1)

time: 50.3 us -> 50.3 us (level)
  no operation moved by 1% of the time
where the time goes in v7:
time: 50.3 us; the launch traced here: 50 us
  Pallas kernels  49.2 us (98%)
  local copies, waits for them, and re-layouts  0.8 us (2%)
    pallas_call x1, Pallas kernels, per_device(): pl.pallas_call(partial(exchange_kernel, outer, inner, heads), out_shape=j...  49.2 us

profile of v7, /device:TPU:0, one launch (start us, length us, event | category | flops | bytes accessed | tf_op | source)
XLA Modules:
  0.0 50.0 jit_solution(1609053077940784253)
XLA Ops:
  0.0 49.2 %shard_map.37 = bf16[32,2,4096]{2,1,0:T(2,128)(2,1)S(1)} custom-call(bf16[128,2,1024]{2,1,0:T(2,128)(2,1)} %q_ref.1, bf16[128,2,1024]{2,1,0:T(2,128)(2,1)} %k_ref.1, bf16[128,2,1024]{2,1,0:T(2,128)(2,1)} %v_ref.1), custom_call_target="tpu_custom_call" | custom-call | tf_op jit(solution)/shard_map/pallas_call | solution.py:390
  49.2 0.8 %copy.5 = bf16[32,2,4096]{2,1,0:T(2,128)(2,1)} copy(bf16[32,2,4096]{2,1,0:T(2,128)(2,1)S(1)} %shard_map.37) | data formatting | bytes 1048576
